TPU v7x, 32 devices: a whole 2x2x4 slice. The times are simulated.
32 devices in a mesh: row: 2 (over core), col: 16 (over z, y, x).
Axes of the slice: x: 2, y: 2, z: 4, core: 2. Of those that a mesh axis runs over, the one named last changes fastest.
Arguments:
- object_in: float32 [2, 2, 512, 4096], P(None, None, 'row', 'col'), may hold values from -4 to 4
- probe_in: float32 [2, 256, 256], replicated, may hold values from -5 to 5
- positions: int32 [2, 16, 2, 2], P('row', 'col'), may hold values from -32 to 32
- intensity: float32 [2, 16, 2, 256, 256], P('row', 'col'), may hold values from 0.1 to 8.2
Outputs:
- object_out: float32 [2, 2, 512, 4096], P(None, None, 'row', 'col')
- probe_out: float32 [2, 256, 256], replicated
Inputs may be any that keep to these rules, and one draw needn't show every extreme that they name: positions[r, c, p] = (dy, dx) places the probe of position p on object rows r * 256 + dy to r * 256 + dy + 255 and columns c * 256 + dx to c * 256 + dx + 255.
All inputs are finite; a program needn't handle non-finite values.
Results may differ from a plain program's by a relative error of at most 0.0003.
Values sent between devices are 32-bit elements; how exact they have to be, the bound alone decides.
No kernel may reach another device: no remote copies, remote signals or barrier semaphores. Data moves between devices by JAX's collectives and lax.ppermute only.
A program may use at most 64 MiB of HBM per device.

v0:
```python
import math
import jax
import jax.numpy as jnp
from jax import lax
from jax.sharding import PartitionSpec as P

RIM = 32


def passed_along(value, axis, steps):
    count = lax.axis_size(axis)
    initial, last = (max(0, -steps), min(count, count - steps))
    return lax.ppermute(value, axis, [(source, source + steps) for source in range(initial, last)])


def extended(cells, sides, width):
    for axis, dim in sides:
        count = lax.axis_size(axis)
        ends = count - 1
        head = lax.slice_in_dim(cells, 0, width, axis=dim)
        tail = lax.slice_in_dim(cells, cells.shape[dim] - width, cells.shape[dim], axis=dim)
        cells = jnp.concatenate(
            [
                lax.ppermute(tail, axis, [(i, (i + 1) % count) for i in range(ends)]),
                cells,
                lax.ppermute(head, axis, [((i + 1) % count, i) for i in range(ends)]),
            ],
            axis=dim,
        )
    return cells


def tables(extent):
    line_idx = jnp.arange(extent, dtype=jnp.int32)
    turn_count = line_idx[:, None] * line_idx[None, :] % extent
    angles = turn_count.astype(jnp.float32) * (2.0 * math.pi / extent)
    factor = 1.0 / math.sqrt(extent)
    cosine = jnp.cos(angles) * factor
    sine_tab = jnp.sin(angles) * factor
    frequency = ((line_idx + extent // 2) % extent - extent // 2).astype(jnp.float32)
    phases = (
        -math.pi * 8.0 / (extent * extent) * (frequency[:, None] ** 2 + frequency[None, :] ** 2)
    )
    return (cosine, sine_tab, jnp.cos(phases), jnp.sin(phases))


def matrices(cosine, sine_tab, orient):
    return (cosine, sine_tab, float(orient))


def transform(real_part, imag_part, tables_pair):
    cosine, sine_tab, orient = tables_pair
    high = lax.Precision.HIGHEST
    rc = jnp.einsum("byx,xk->byk", real_part, cosine, precision=high)
    rs = jnp.einsum("byx,xk->byk", real_part, sine_tab, precision=high)
    ic = jnp.einsum("byx,xk->byk", imag_part, cosine, precision=high)
    isn = jnp.einsum("byx,xk->byk", imag_part, sine_tab, precision=high)
    mid_re = rc + orient * isn
    mid_im = ic - orient * rs
    out_re = jnp.einsum("ky,byx->bkx", cosine, mid_re, precision=high) + orient * jnp.einsum(
        "ky,byx->bkx", sine_tab, mid_im, precision=high
    )
    out_im = jnp.einsum("ky,byx->bkx", cosine, mid_im, precision=high) - orient * jnp.einsum(
        "ky,byx->bkx", sine_tab, mid_re, precision=high
    )
    return (out_re, out_im)


def times_plain(first_re, first_im, second_re, second_im):
    return (
        first_re * second_re - first_im * second_im,
        first_re * second_im + first_im * second_re,
    )


def times_conj(first_re, first_im, second_re, second_im):
    return (
        first_re * second_re + first_im * second_im,
        first_re * second_im - first_im * second_re,
    )


def tile_gradient(window, probe, offsets, measured, constants):
    cosine, sine_tab, kern_re, kern_im = constants
    forward = matrices(cosine, sine_tab, 1)
    backward = matrices(cosine, sine_tab, -1)
    extent = probe.shape[-1]
    zero_idx = jnp.zeros((), jnp.int32)

    def cut_patch(offset):
        return lax.dynamic_slice(
            window, (zero_idx, zero_idx, offset[0] + RIM, offset[1] + RIM), (2, 2, extent, extent)
        )

    patches = jax.vmap(cut_patch)(offsets)
    first_re, first_im = (patches[:, 0, 0], patches[:, 0, 1])
    second_re, second_im = (patches[:, 1, 0], patches[:, 1, 1])
    probe_re, probe_im = (probe[0], probe[1])
    wave_re, wave_im = times_plain(probe_re, probe_im, first_re, first_im)
    spec_re, spec_im = transform(wave_re, wave_im, forward)
    spec_re, spec_im = times_plain(kern_re, kern_im, spec_re, spec_im)
    prop_re, prop_im = transform(spec_re, spec_im, backward)
    exit_re, exit_im = times_plain(prop_re, prop_im, second_re, second_im)
    far_re, far_im = transform(exit_re, exit_im, forward)
    excess = 2.0 * (far_re * far_re + far_im * far_im - measured)
    back_re, back_im = transform(excess * far_re, excess * far_im, backward)
    grad2_re, grad2_im = times_conj(prop_re, prop_im, back_re, back_im)
    lift_re, lift_im = times_conj(second_re, second_im, back_re, back_im)
    lift_re, lift_im = transform(lift_re, lift_im, forward)
    lift_re, lift_im = times_conj(kern_re, kern_im, lift_re, lift_im)
    enter_re, enter_im = transform(lift_re, lift_im, backward)
    grad1_re, grad1_im = times_conj(probe_re, probe_im, enter_re, enter_im)
    probe_re_g, probe_im_g = times_conj(first_re, first_im, enter_re, enter_im)
    probe_grad = jnp.stack([jnp.sum(probe_re_g, 0), jnp.sum(probe_im_g, 0)], 0)
    pieces = jnp.stack([jnp.stack([grad1_re, grad1_im], 1), jnp.stack([grad2_re, grad2_im], 1)], 1)
    gradient = jnp.zeros(window.shape, jnp.float32)
    for position in range(offsets.shape[0]):
        start_at = (zero_idx, zero_idx, offsets[position, 0] + RIM, offsets[position, 1] + RIM)
        current = lax.dynamic_slice(gradient, start_at, pieces.shape[1:])
        gradient = lax.dynamic_update_slice(gradient, current + pieces[position], start_at)
    return (gradient, probe_grad)


def turned(block):
    return jnp.swapaxes(block, 2, 3)


def rows_then_cols(gradient):
    inner_px = gradient.shape[-1] - 2 * RIM
    upper_end = RIM + inner_px
    from_below = passed_along(gradient[:, :, :RIM, :], "row", -1)
    from_above = passed_along(gradient[:, :, upper_end:, :], "row", 1)
    middle = gradient[:, :, RIM:upper_end, :]
    middle = middle.at[:, :, inner_px - RIM :, :].add(from_below)
    middle = middle.at[:, :, :RIM, :].add(from_above)
    from_right = turned(passed_along(turned(middle[..., :RIM]), "col", -1))
    from_left = turned(passed_along(turned(middle[..., upper_end:]), "col", 1))
    interior = middle[..., RIM:upper_end]
    interior = interior.at[..., inner_px - RIM :].add(from_right)
    interior = interior.at[..., :RIM].add(from_left)
    return interior


def local(object_in, probe_in, positions, intensity):
    extent = probe_in.shape[-1]
    constants = tables(extent)
    offsets = positions.reshape(-1, 2)
    measured = intensity.reshape(-1, extent, extent)
    tile_total = lax.axis_size("row") * lax.axis_size("col")
    probe_rate = 2.0 / tile_total
    current = object_in
    window = extended(current, (("row", 2), ("col", 3)), RIM)
    gradient, probe_grad = tile_gradient(window, probe_in, offsets, measured, constants)
    probe_total = lax.psum(probe_grad, ("row", "col"))
    probe_next = probe_in - probe_rate * probe_total
    descent = rows_then_cols(gradient)
    local_peak = jnp.max(descent[:, 0] ** 2 + descent[:, 1] ** 2)
    largest = lax.pmax(local_peak, ("row", "col"))
    current = current - 0.3 * descent / (jnp.sqrt(largest) + 1e-06)
    return (current, probe_next)


def solution(mesh):
    placed = (
        P(None, None, "row", "col"),
        P(),
        P("row", "col", None, None),
        P("row", "col", None, None, None),
    )
    return jax.shard_map(
        local,
        mesh=mesh,
        in_specs=placed,
        out_specs=(P(None, None, "row", "col"), P()),
        check_vma=False,
    )
```

profile of v0, /device:TPU:0, one launch (start us, length us, event | category | flops | bytes accessed | tf_op | source)
XLA Modules:
  0.0 372.2 jit_solution(18278796465916017940)
XLA Ops:
  10.1 2.4 collective-permute-start
  22.2 2.0 copy.98
  24.5 4.2 %collective-permute-start.2 = (f32[2,2,320,32]{2,3,1,0:T(8,128)S(1)}, f32[2,2,320,32]{2,3,1,0:T(8,128)S(1)}, u32[]{:S(2)}, u32[]{:S(2)}) collective-permute-start(f32[2,2,320,32]{2,3,1,0:T(8,128)S(1)} %get-tuple-element.84), channel_id=1, source_target_pairs={{0,1},{1,2},{2,3},{3,4},{4,5},{5,6},{6,7},{7,8},{8,9},{9,10},{10,1... | collective-permute-start | bytes 491528 | tf_op jit(solution)/shard_map/ppermute | solution.py:24
  30.1 3.7 collective-permute-done.2
  33.8 6.2 %collective-permute-done.3 = f32[2,2,320,32]{2,3,1,0:T(8,128)S(1)} collective-permute-done((f32[2,2,320,32]{2,3,1,0:T(8,128)S(1)}, f32[2,2,320,32]{2,3,1,0:T(8,128)S(1)}, u32[]{:S(2)}, u32[]{:S(2)}) %collective-permute-start.3) | collective-permute-done | bytes 163872 | tf_op jit(solution)/shard_map/ppermute | solution.py:26
  41.8 11.3 %while.5 = (s32[]{:T(128)}, f32[2,2,320,320]{2,3,1,0:T(8,128)S(1)}, s32[2,4]{1,0:T(2,128)S(1)}, f32[2,2,2,256,256]{3,4,0,2,1:T(8,128)}, s32[]{:T(128)}) while((s32[]{:T(128)}, f32[2,2,320,320]{2,3,1,0:T(8,128)S(1)}, s32[2,4]{1,0:T(2,128)S(1)}, f32[2,2,2,256,256]{3,4,0,2,1:T(8,128)}, s32[]{:T(128)}) %tuple.62), condition=%wide.while_cond.4, body=%wide.while_body.4.sunk | while | flops 2 | bytes 21496496 | solution.py:91
  53.1 3.4 fusion.112
  56.5 3.2 fusion.116
  59.8 1.9 convolution_subtract_fusion.5
  63.5 1.9 convolution_add_fusion.5
  65.4 1.8 fusion.114
  67.2 2.3 fusion.22
  69.5 1.8 fusion.23
  71.4 1.9 fusion.108
  73.3 1.9 fusion.104
  75.1 1.9 fusion.21
  77.0 1.8 fusion.106
  78.8 2.1 fusion.20
  80.9 1.8 fusion.102
  82.7 1.8 fusion.17
  84.6 1.9 fusion.32
  86.5 1.8 fusion.100
  88.3 1.8 fusion.96
  90.1 2.0 convolution_add_fusion.3
  92.2 1.8 fusion.98
  94.0 1.8 convolution_subtract_fusion.3
  95.9 1.8 fusion.94
  97.7 1.8 fusion.15
  99.6 1.8 fusion.14
  101.4 1.9 fusion.92
  103.3 2.3 fusion.88
  105.7 1.9 fusion.13
  107.6 1.9 fusion.12
  109.6 1.8 fusion.86
  111.4 1.8 fusion.90
  113.2 1.8 fusion.9
  115.1 2.2 add_bitcast_fusion
  117.2 1.8 fusion.80
  119.0 1.8 fusion.84
  120.9 1.9 convolution_subtract_fusion.1
  122.8 1.8 fusion.78
  124.6 1.8 convolution_add_fusion.1
  126.4 2.1 fusion.82
  128.5 1.8 fusion.6
  130.4 1.8 fusion.7
  132.2 1.9 fusion.76
  134.1 1.9 fusion.72
  136.0 1.9 fusion.5
  137.9 2.3 fusion.4
  140.1 1.8 fusion.70
  142.0 1.8 fusion.74
  143.8 1.8 fusion.1
  145.6 2.8 fusion.38
  150.1 13.4 %dynamic_update_slice.6 = f32[2,2,320,320]{2,3,1,0:T(8,128)S(1)} dynamic-update-slice(f32[2,2,320,320]{2,3,1,0:T(8,128)S(1)} %broadcast_in_dim.2, f32[2,2,256,256]{2,3,1,0:T(8,128)} %fusion.25, s32[]{:T(128)} %constant.162.clone.1, s32[]{:T(128)} %constant.162.clone.1, s32[]{:T(128)S(6)} %select_n.155, s32[]{:T(128)S(6)} %select_n.156) | dynamic-update-slice | bytes 2097156 | tf_op jit(solution)/shard_map/dynamic_update_slice | solution.py:120
  163.5 2.4 fusion.27
  165.9 14.0 %dynamic_update_slice.7 = f32[2,2,320,320]{2,3,1,0:T(8,128)S(1)} dynamic-update-slice(f32[2,2,320,320]{2,3,1,0:T(8,128)S(1)} %dynamic_update_slice.6, f32[2,2,256,256]{2,3,1,0:T(8,128)} %fusion.27, s32[]{:T(128)} %constant.162.clone.1, s32[]{:T(128)} %constant.162.clone.1, s32[]{:T(128)S(6)} %select_n.157, s32[]{:T(128)S(6)} %select_n.158) | dynamic-update-slice | bytes 2097156 | tf_op jit(solution)/shard_map/dynamic_update_slice | solution.py:120
  181.8 2.0 copy.129
  187.1 4.4 %collective-permute-start.5 = (f32[2,2,32,320]{3,2,1,0:T(8,128)}, f32[2,2,32,320]{3,2,1,0:T(8,128)}, u32[]{:S(2)}, u32[]{:S(2)}) collective-permute-start(f32[2,2,32,320]{3,2,1,0:T(8,128)} %copy.126), channel_id=1, source_target_pairs={{0,16},{1,17},{2,18},{3,19},{4,20},{5,21},{6,22},{7,23},{8,24},{9,... | collective-permute-start | bytes 491528 | tf_op jit(solution)/shard_map/ppermute | solution.py:13
  192.8 3.7 %scatter-add.14 = f32[2,2,256,320]{2,3,1,0:T(8,128)} dynamic-update-slice(f32[2,2,256,320]{2,3,1,0:T(8,128)} %slice.249, f32[2,2,32,320]{2,3,1,0:T(8,128)S(1)} %slice_add_fusion.1, s32[]{:T(128)} %constant.162.clone.1, s32[]{:T(128)} %constant.162.clone.1, s32[]{:T(128)} %constant.175.clone.1, s32[]{:T(128)} %constant.162.clone.1) | dynamic-update-slice | bytes 327684 | tf_op jit(solution)/shard_map/scatter-add | solution.py:134
  198.8 3.6 scatter-add.15
  206.8 4.7 %collective-permute-start.7 = (f32[2,2,32,256]{3,2,1,0:T(8,128)S(1)}, f32[2,2,32,256]{3,2,1,0:T(8,128)S(1)}, u32[]{:S(2)}, u32[]{:S(2)}) collective-permute-start(f32[2,2,32,256]{3,2,1,0:T(8,128)S(1)} %get-tuple-element.90), channel_id=1, source_target_pairs={{0,1},{1,2},{2,3},{3,4},{4,5},{5,6},{6,7},{7,8},{8,9},{9,10},{10,1... | collective-permute-start | bytes 393224 | tf_op jit(solution)/shard_map/ppermute | solution.py:13
  211.5 105.9 %all-reduce.2.cloned.1.call-done = f32[2,256,256]{1,2,0:T(8,128)} async-done(((f32[2,256,256]{1,2,0:T(8,128)}), f32[2,256,256]{1,2,0:T(8,128)}) %all-reduce.2.cloned.1.call-update) | async-done | bytes 524304 | tf_op jit(solution)/shard_map/psum | solution.py:154
  321.3 39.5 %pmax.7 = f32[]{:T(128)} all-reduce(f32[]{:T(128)} %fusion.29), channel_id=1, replica_groups=mesh['row'=2,'col'=16] {'row','col'}, use_global_device_ids=true, to_apply=%region_1.2 | all-reduce | flops 1 | bytes 8 | tf_op jit(solution)/shard_map/pmax | solution.py:158
  362.6 2.5 copy.130
  (97 shorter events, 43.4 us)
Async XLA Ops:
  7.2 6.7 %copy-start.15 = (s32[1,1,2,2]{3,2,1,0:T(2,128)S(1)}, s32[1,1,2,2]{3,2,1,0:T(2,128)}, u32[]{:S(2)}) copy-start(s32[1,1,2,2]{3,2,1,0:T(2,128)} %param.14) | copy-start | bytes 52
  7.2 12.2 %copy-start.12 = (f32[2,256,256]{2,1,0:T(8,128)S(1)}, f32[2,256,256]{2,1,0:T(8,128)}, u32[]{:S(2)}) copy-start(f32[2,256,256]{2,1,0:T(8,128)} %param.13) | copy-start | bytes 1572868
  7.2 310.2 %all-reduce.2.cloned.1.call-start = ((), (), s32[]{:S(2)}) async-start(), calls=%async_computation | async-start | bytes 1048576 | tf_op jit(solution)/shard_map/psum | solution.py:154
  8.8 31.1 %copy-start.2 = (f32[2,2,256,256]{2,3,1,0:T(8,128)}, f32[2,2,256,256]{2,3,1,0:T(8,128)S(1)}, u32[]{:S(2)}) copy-start(f32[2,2,256,256]{2,3,1,0:T(8,128)S(1)} %copy.128) | copy-start | bytes 3145732
  10.1 14.2 %collective-permute-start = (f32[2,2,32,256]{2,3,1,0:T(8,128)}, f32[2,2,32,256]{2,3,1,0:T(8,128)S(1)}, u32[]{:S(2)}, u32[]{:S(2)}) collective-permute-start(f32[2,2,32,256]{2,3,1,0:T(8,128)} %get-tuple-element.96), channel_id=1, source_target_pairs={{0,16},{1,17},{2,18},{3,19},{4,20},{5,21},{6,22},{7,23},{8,24},{9,... | collective-permute-start | bytes 393224 | tf_op jit(solution)/shard_map/ppermute | solution.py:24
  12.5 11.7 %collective-permute-start.1 = (f32[2,2,32,256]{2,3,1,0:T(8,128)}, f32[2,2,32,256]{2,3,1,0:T(8,128)S(1)}, u32[]{:S(2)}, u32[]{:S(2)}) collective-permute-start(f32[2,2,32,256]{2,3,1,0:T(8,128)} %get-tuple-element.97), channel_id=1, source_target_pairs={{16,0},{17,1},{18,2},{19,3},{20,4},{21,5},{22,6},{23,7},{24,8},{25... | collective-permute-start | bytes 393224 | tf_op jit(solution)/shard_map/ppermute | solution.py:26
  24.3 9.5 %copy-start.9 = (f32[2,2,32,256]{2,3,1,0:T(8,128)}, f32[2,2,32,256]{2,3,1,0:T(8,128)S(1)}, u32[]{:S(2)}) copy-start(f32[2,2,32,256]{2,3,1,0:T(8,128)S(1)} %collective-permute-done) | copy-start | bytes 393220
  24.3 9.5 %copy-start.10 = (f32[2,2,32,256]{2,3,1,0:T(8,128)}, f32[2,2,32,256]{2,3,1,0:T(8,128)S(1)}, u32[]{:S(2)}) copy-start(f32[2,2,32,256]{2,3,1,0:T(8,128)S(1)} %collective-permute-done.1) | copy-start | bytes 393220
  24.5 9.3 %collective-permute-start.2 = (f32[2,2,320,32]{2,3,1,0:T(8,128)S(1)}, f32[2,2,320,32]{2,3,1,0:T(8,128)S(1)}, u32[]{:S(2)}, u32[]{:S(2)}) collective-permute-start(f32[2,2,320,32]{2,3,1,0:T(8,128)S(1)} %get-tuple-element.84), channel_id=1, source_target_pairs={{0,1},{1,2},{2,3},{3,4},{4,5},{5,6},{6,7},{7,8},{8,9},{9,10},{10,1... | collective-permute-start | bytes 491528 | tf_op jit(solution)/shard_map/ppermute | solution.py:24
  28.7 11.2 %collective-permute-start.3 = (f32[2,2,320,32]{2,3,1,0:T(8,128)S(1)}, f32[2,2,320,32]{2,3,1,0:T(8,128)S(1)}, u32[]{:S(2)}, u32[]{:S(2)}) collective-permute-start(f32[2,2,320,32]{2,3,1,0:T(8,128)S(1)} %get-tuple-element.85), channel_id=1, source_target_pairs={{1,0},{2,1},{3,2},{4,3},{5,4},{6,5},{7,6},{8,7},{9,8},{10,9},{11,1... | collective-permute-start | bytes 491528 | tf_op jit(solution)/shard_map/ppermute | solution.py:26
  41.8 1.3 copy-start
  45.4 1.9 copy-start.1
  47.3 1.3 copy-start
  50.9 1.9 copy-start.1
  53.1 6.6 %copy-start.6 = (f32[256,256]{0,1:T(8,128)S(1)}, f32[256,256]{0,1:T(8,128)}, u32[]{:S(2)}) copy-start(f32[256,256]{0,1:T(8,128)} %copy.64) | copy-start | bytes 786436
  53.1 6.6 %copy-start.7 = (f32[256,256]{0,1:T(8,128)S(1)}, f32[256,256]{0,1:T(8,128)}, u32[]{:S(2)}) copy-start(f32[256,256]{0,1:T(8,128)} %copy.71) | copy-start | bytes 786436
  53.1 6.6 %copy-start.8 = (f32[2,2,2,256,256]{3,4,0,2,1:T(8,128)S(1)}, f32[2,2,2,256,256]{3,4,0,2,1:T(8,128)}, u32[]{:S(2)}) copy-start(f32[2,2,2,256,256]{3,4,0,2,1:T(8,128)} %get-tuple-element.57) | copy-start | bytes 6291460
  95.9 5.5 %copy-start.4 = (f32[1,1,2,256,256]{3,4,2,1,0:T(8,128)S(1)}, f32[1,1,2,256,256]{3,4,2,1,0:T(8,128)}, u32[]{:S(2)}) copy-start(f32[1,1,2,256,256]{3,4,2,1,0:T(8,128)} %copy.98) | copy-start | bytes 1572868
  148.6 1.3 copy-start.5
  180.4 5.0 %copy-start.13 = (f32[256,256]{0,1:T(8,128)S(1)}, f32[256,256]{0,1:T(8,128)}, u32[]{:S(2)}) copy-start(f32[256,256]{0,1:T(8,128)} %get-tuple-element.66) | copy-start | bytes 786436
  180.4 5.0 %copy-start.14 = (f32[256,256]{0,1:T(8,128)S(1)}, f32[256,256]{0,1:T(8,128)}, u32[]{:S(2)}) copy-start(f32[256,256]{0,1:T(8,128)} %get-tuple-element.67) | copy-start | bytes 786436
  180.4 11.1 %collective-permute-start.4 = (f32[2,2,32,320]{3,2,1,0:T(8,128)S(1)}, f32[2,2,32,320]{3,2,1,0:T(8,128)}, u32[]{:S(2)}, u32[]{:S(2)}) collective-permute-start(f32[2,2,32,320]{3,2,1,0:T(8,128)S(1)} %copy.124), channel_id=1, source_target_pairs={{16,0},{17,1},{18,2},{19,3},{20,4},{21,5},{22,6},{23,7},{24,8},{25... | collective-permute-start | bytes 491528 | tf_op jit(solution)/shard_map/ppermute | solution.py:13
  187.1 9.4 %collective-permute-start.5 = (f32[2,2,32,320]{3,2,1,0:T(8,128)}, f32[2,2,32,320]{3,2,1,0:T(8,128)}, u32[]{:S(2)}, u32[]{:S(2)}) collective-permute-start(f32[2,2,32,320]{3,2,1,0:T(8,128)} %copy.126), channel_id=1, source_target_pairs={{0,16},{1,17},{2,18},{3,19},{4,20},{5,21},{6,22},{7,23},{8,24},{9,... | collective-permute-start | bytes 491528 | tf_op jit(solution)/shard_map/ppermute | solution.py:13
  198.8 118.5 %copy-start.11 = (f32[2,256,256]{1,2,0:T(8,128)S(1)}, f32[2,256,256]{1,2,0:T(8,128)}, u32[]{:S(2)}) copy-start(f32[2,256,256]{1,2,0:T(8,128)} %copy.129) | copy-start | bytes 1572868
  205.5 113.0 %collective-permute-start.6 = (f32[2,2,32,256]{3,2,1,0:T(8,128)}, f32[2,2,32,256]{3,2,1,0:T(8,128)S(1)}, u32[]{:S(2)}, u32[]{:S(2)}) collective-permute-start(f32[2,2,32,256]{3,2,1,0:T(8,128)} %get-tuple-element.91), channel_id=1, source_target_pairs={{1,0},{2,1},{3,2},{4,3},{5,4},{6,5},{7,6},{8,7},{9,8},{10,9},{11,1... | collective-permute-start | bytes 393224 | tf_op jit(solution)/shard_map/ppermute | solution.py:13
  206.8 154.7 %copy-start.3 = (f32[2,2,256,256]{2,3,1,0:T(8,128)S(1)}, f32[2,2,256,256]{2,3,1,0:T(8,128)}, u32[]{:S(2)}) copy-start(f32[2,2,256,256]{2,3,1,0:T(8,128)} %copy-done.2) | copy-start | bytes 3145732
  206.8 112.6 %collective-permute-start.7 = (f32[2,2,32,256]{3,2,1,0:T(8,128)S(1)}, f32[2,2,32,256]{3,2,1,0:T(8,128)S(1)}, u32[]{:S(2)}, u32[]{:S(2)}) collective-permute-start(f32[2,2,32,256]{3,2,1,0:T(8,128)S(1)} %get-tuple-element.90), channel_id=1, source_target_pairs={{0,1},{1,2},{2,3},{3,4},{4,5},{5,6},{6,7},{7,8},{8,9},{9,10},{10,1... | collective-permute-start | bytes 393224 | tf_op jit(solution)/shard_map/ppermute | solution.py:13
Sparse Core Ops, SparseCore 0:
  186.3 130.9 all-reduce.1
where the time goes:
time: 377 us; the launch traced here: 372 us
  waiting for transfers between devices  116 us (31%)
  matrix products  94.9 us (25%)
  local copies, waits for them, and re-layouts  67.2 us (18%)
  blocking collectives  39.5 us (10%)
  starting transfers between devices  21 us (6%)
  between operations  20.6 us (5%)
  other arithmetic  12.9 us (3%)
    psum x1, waiting for transfers between devices, local(): probe_total = lax.psum(probe_grad, ('row', 'col'))  106 us
    pmax x1, blocking collectives, local(): largest = lax.pmax(local_peak, ('row', 'col'))  39.5 us
    dynamic_update_slice x2, local copies, waits for them, and re-layouts, tile_gradient(): lax.dynamic_update_slice(gradient, current + pieces[position], start_at)  27.5 us
    dot_general x6, matrix products, transform(): ic = jnp.einsum('byx,xk->byk', imag_part, cosine, precision=high)  13.1 us
    dot_general x6, matrix products, transform(): rc = jnp.einsum('byx,xk->byk', real_part, cosine, precision=high)  12.6 us
    dot_general x6, matrix products, transform(): jnp.einsum('ky,byx->bkx', sine_tab, mid_im, precision=high)  12.4 us
    dot_general x6, matrix products, transform(): rs = jnp.einsum('byx,xk->byk', real_part, sine_tab, precision=high)  11.8 us
    ppermute x4, starting transfers between devices, passed_along(): lax.ppermute(value, axis, [(source, source + steps) for source in range(i...  11.8 us
  transfers between devices with their start and end apart: 9, of which 3 were waited for; matrix products, arithmetic and copies ran while one was open for 7% of the time, Pallas kernels for 0%

commit v1 on v0

--- a/solution.py
+++ b/solution.py
@@ -151,7 +151,7 @@
     current = object_in
     window = extended(current, (("row", 2), ("col", 3)), RIM)
     gradient, probe_grad = tile_gradient(window, probe_in, offsets, measured, constants)
-    probe_total = lax.psum(probe_grad, ("row", "col"))
+    probe_total = lax.psum(lax.psum(probe_grad, "col"), "row")
     probe_next = probe_in - probe_rate * probe_total
     descent = rows_then_cols(gradient)
     local_peak = jnp.max(descent[:, 0] ** 2 + descent[:, 1] ** 2)

time: 377 us -> 356 us (0.944)
  waiting for transfers between devices: 116 us -> 97 us
    psum x1 -> x2, waiting for transfers between devices: 106 us -> 86.3 us  [local(): probe_total = lax.psum(lax.psum(probe_grad, 'col'), 'row')]
    unnamed x33 -> x29, local copies, waits for them, and re-layouts: 9.49 us -> 8.22 us
  transfers between devices with their start and end apart: 9 -> 10, of which waited for: 3 -> 4; matrix products, arithmetic and copies ran while one was open for 7% -> 8% of each run, Pallas kernels for 0% -> 0%
where the time goes in v1:
time: 356 us; the launch traced here: 351 us
  waiting for transfers between devices  97 us (27%)
  matrix products  94.8 us (27%)
  local copies, waits for them, and re-layouts  65.3 us (18%)
  blocking collectives  39.5 us (11%)
  starting transfers between devices  20.9 us (6%)
  between operations  20.6 us (6%)
  other arithmetic  12.8 us (4%)
    psum x2, waiting for transfers between devices, local(): probe_total = lax.psum(lax.psum(probe_grad, 'col'), 'row')  86.3 us
    pmax x1, blocking collectives, local(): largest = lax.pmax(local_peak, ('row', 'col'))  39.5 us
    dynamic_update_slice x2, local copies, waits for them, and re-layouts, tile_gradient(): lax.dynamic_update_slice(gradient, current + pieces[position], start_at)  27.5 us
    dot_general x6, matrix products, transform(): ic = jnp.einsum('byx,xk->byk', imag_part, cosine, precision=high)  13.1 us
    dot_general x6, matrix products, transform(): rc = jnp.einsum('byx,xk->byk', real_part, cosine, precision=high)  12.6 us
    dot_general x6, matrix products, transform(): jnp.einsum('ky,byx->bkx', sine_tab, mid_im, precision=high)  12.2 us
    dot_general x6, matrix products, transform(): rs = jnp.einsum('byx,xk->byk', real_part, sine_tab, precision=high)  11.8 us
    ppermute x4, starting transfers between devices, passed_along(): lax.ppermute(value, axis, [(source, source + steps) for source in range(i...  11.6 us
  transfers between devices with their start and end apart: 10, of which 4 were waited for; matrix products, arithmetic and copies ran while one was open for 8% of the time, Pallas kernels for 0%

profile of v1, /device:TPU:0, one launch (start us, length us, event | category | flops | bytes accessed | tf_op | source)
XLA Modules:
  0.0 351.2 jit_solution(4191340781180632826)
XLA Ops:
  10.1 2.4 collective-permute-start
  22.3 2.0 copy.98
  24.6 4.2 %collective-permute-start.2 = (f32[2,2,320,32]{2,3,1,0:T(8,128)S(1)}, f32[2,2,320,32]{2,3,1,0:T(8,128)S(1)}, u32[]{:S(2)}, u32[]{:S(2)}) collective-permute-start(f32[2,2,320,32]{2,3,1,0:T(8,128)S(1)} %get-tuple-element.84), channel_id=1, source_target_pairs={{0,1},{1,2},{2,3},{3,4},{4,5},{5,6},{6,7},{7,8},{8,9},{9,10},{10,1... | collective-permute-start | bytes 491528 | tf_op jit(solution)/shard_map/ppermute | solution.py:24
  30.2 3.7 %collective-permute-done.2 = f32[2,2,320,32]{2,3,1,0:T(8,128)S(1)} collective-permute-done((f32[2,2,320,32]{2,3,1,0:T(8,128)S(1)}, f32[2,2,320,32]{2,3,1,0:T(8,128)S(1)}, u32[]{:S(2)}, u32[]{:S(2)}) %collective-permute-start.2) | collective-permute-done | bytes 163872 | tf_op jit(solution)/shard_map/ppermute | solution.py:24
  33.9 6.2 %collective-permute-done.3 = f32[2,2,320,32]{2,3,1,0:T(8,128)S(1)} collective-permute-done((f32[2,2,320,32]{2,3,1,0:T(8,128)S(1)}, f32[2,2,320,32]{2,3,1,0:T(8,128)S(1)}, u32[]{:S(2)}, u32[]{:S(2)}) %collective-permute-start.3) | collective-permute-done | bytes 163872 | tf_op jit(solution)/shard_map/ppermute | solution.py:26
  41.9 11.4 %while.5 = (s32[]{:T(128)}, f32[2,2,320,320]{2,3,1,0:T(8,128)S(1)}, s32[2,4]{1,0:T(2,128)S(1)}, f32[2,2,2,256,256]{3,4,0,2,1:T(8,128)}, s32[]{:T(128)}) while((s32[]{:T(128)}, f32[2,2,320,320]{2,3,1,0:T(8,128)S(1)}, s32[2,4]{1,0:T(2,128)S(1)}, f32[2,2,2,256,256]{3,4,0,2,1:T(8,128)}, s32[]{:T(128)}) %tuple.62), condition=%wide.while_cond.4, body=%wide.while_body.4.sunk | while | flops 2 | bytes 21496496 | solution.py:91
  53.4 3.4 fusion.112
  56.7 3.2 fusion.116
  60.0 1.9 convolution_subtract_fusion.5
  61.9 1.8 fusion.110
  63.7 1.9 convolution_add_fusion.5
  65.6 1.8 fusion.114
  67.4 2.3 fusion.22
  69.8 1.8 fusion.23
  71.6 1.9 fusion.108
  73.5 1.9 fusion.104
  75.4 1.9 fusion.21
  79.1 2.1 fusion.20
  81.1 1.8 fusion.102
  82.9 1.8 fusion.17
  84.8 1.9 fusion.32
  86.6 1.8 fusion.100
  88.5 1.8 fusion.96
  90.3 2.1 convolution_add_fusion.3
  92.4 1.8 fusion.98
  94.2 1.8 convolution_subtract_fusion.3
  96.1 1.8 fusion.94
  97.9 1.8 fusion.15
  99.7 1.8 fusion.14
  101.6 1.9 fusion.92
  103.5 2.3 fusion.88
  105.8 1.9 fusion.13
  107.8 1.9 fusion.12
  109.7 1.8 fusion.86
  111.6 1.8 fusion.90
  113.4 1.8 fusion.9
  115.2 2.1 add_bitcast_fusion
  117.4 1.8 fusion.80
  119.2 1.8 fusion.84
  121.1 1.9 convolution_subtract_fusion.1
  122.9 1.8 fusion.78
  124.8 1.9 convolution_add_fusion.1
  126.6 2.1 fusion.82
  128.7 1.8 fusion.6
  130.5 1.8 fusion.7
  132.4 1.9 fusion.76
  134.3 1.9 fusion.72
  136.2 1.9 fusion.5
  138.1 2.3 fusion.4
  140.3 1.8 fusion.70
  144.0 1.8 fusion.1
  145.8 2.7 fusion.38
  150.2 13.5 %dynamic_update_slice.6 = f32[2,2,320,320]{2,3,1,0:T(8,128)S(1)} dynamic-update-slice(f32[2,2,320,320]{2,3,1,0:T(8,128)S(1)} %broadcast_in_dim.2, f32[2,2,256,256]{2,3,1,0:T(8,128)} %fusion.25, s32[]{:T(128)} %constant.162.clone.1, s32[]{:T(128)} %constant.162.clone.1, s32[]{:T(128)S(6)} %select_n.155, s32[]{:T(128)S(6)} %select_n.156) | dynamic-update-slice | bytes 2097156 | tf_op jit(solution)/shard_map/dynamic_update_slice | solution.py:120
  163.6 2.4 fusion.27
  166.0 14.0 %dynamic_update_slice.7 = f32[2,2,320,320]{2,3,1,0:T(8,128)S(1)} dynamic-update-slice(f32[2,2,320,320]{2,3,1,0:T(8,128)S(1)} %dynamic_update_slice.6, f32[2,2,256,256]{2,3,1,0:T(8,128)} %fusion.27, s32[]{:T(128)} %constant.162.clone.1, s32[]{:T(128)} %constant.162.clone.1, s32[]{:T(128)S(6)} %select_n.157, s32[]{:T(128)S(6)} %select_n.158) | dynamic-update-slice | bytes 2097156 | tf_op jit(solution)/shard_map/dynamic_update_slice | solution.py:120
  186.9 4.4 %collective-permute-start.5 = (f32[2,2,32,320]{3,2,1,0:T(8,128)S(1)}, f32[2,2,32,320]{3,2,1,0:T(8,128)}, u32[]{:S(2)}, u32[]{:S(2)}) collective-permute-start(f32[2,2,32,320]{3,2,1,0:T(8,128)S(1)} %copy.126), channel_id=1, source_target_pairs={{0,16},{1,17},{2,18},{3,19},{4,20},{5,21},{6,22},{7,23},{8,24},{9,... | collective-permute-start | bytes 491528 | tf_op jit(solution)/shard_map/ppermute | solution.py:13
  191.3 2.0 copy.125
  193.3 2.0 slice_add_fusion.1
  195.3 4.3 %scatter-add.14 = f32[2,2,256,320]{2,3,1,0:T(8,128)S(1)} dynamic-update-slice(f32[2,2,256,320]{2,3,1,0:T(8,128)S(1)} %slice.249, f32[2,2,32,320]{2,3,1,0:T(8,128)} %slice_add_fusion.1, s32[]{:T(128)} %constant.162.clone.1, s32[]{:T(128)} %constant.162.clone.1, s32[]{:T(128)} %constant.175.clone.1, s32[]{:T(128)} %constant.162.clone.1) | dynamic-update-slice | bytes 327684 | tf_op jit(solution)/shard_map/scatter-add | solution.py:134
  200.9 2.7 scatter-add.15
  205.7 4.7 %collective-permute-start.7 = (f32[2,2,32,256]{3,2,1,0:T(8,128)}, f32[2,2,32,256]{3,2,1,0:T(8,128)S(1)}, u32[]{:S(2)}, u32[]{:S(2)}) collective-permute-start(f32[2,2,32,256]{3,2,1,0:T(8,128)} %get-tuple-element.90), channel_id=1, source_target_pairs={{0,1},{1,2},{2,3},{3,4},{4,5},{5,6},{6,7},{7,8},{8,9},{9,10},{10,1... | collective-permute-start | bytes 393224 | tf_op jit(solution)/shard_map/ppermute | solution.py:13
  211.2 86.3 %all-reduce.3.cloned.1.call-done = f32[2,256,256]{1,2,0:T(8,128)} async-done(((f32[2,256,256]{1,2,0:T(8,128)}), f32[2,256,256]{1,2,0:T(8,128)}) %all-reduce.3.cloned.1.call-update) | async-done | bytes 524304 | tf_op jit(solution)/shard_map/psum | solution.py:154
  298.4 2.0 copy.129
  300.4 39.5 %pmax.7 = f32[]{:T(128)} all-reduce(f32[]{:T(128)} %fusion.29), channel_id=1, replica_groups=mesh['row'=2,'col'=16] {'row','col'}, use_global_device_ids=true, to_apply=%region_1.2 | all-reduce | flops 1 | bytes 8 | tf_op jit(solution)/shard_map/pmax | solution.py:158
  (96 shorter events, 42.7 us)
Async XLA Ops:
  7.2 6.7 %copy-start.13 = (s32[1,1,2,2]{3,2,1,0:T(2,128)S(1)}, s32[1,1,2,2]{3,2,1,0:T(2,128)}, u32[]{:S(2)}) copy-start(s32[1,1,2,2]{3,2,1,0:T(2,128)} %param.14) | copy-start | bytes 52
  7.2 12.3 %copy-start.12 = (f32[2,256,256]{2,1,0:T(8,128)S(1)}, f32[2,256,256]{2,1,0:T(8,128)}, u32[]{:S(2)}) copy-start(f32[2,256,256]{2,1,0:T(8,128)} %param.13) | copy-start | bytes 1572868
  7.2 290.3 %all-reduce.3.cloned.1.call-start = ((), (), s32[]{:S(2)}) async-start(), calls=%async_computation | async-start | bytes 1048576 | tf_op jit(solution)/shard_map/psum | solution.py:154
  8.8 31.2 %copy-start.2 = (f32[2,2,256,256]{2,3,1,0:T(8,128)}, f32[2,2,256,256]{2,3,1,0:T(8,128)S(1)}, u32[]{:S(2)}) copy-start(f32[2,2,256,256]{2,3,1,0:T(8,128)S(1)} %copy.128) | copy-start | bytes 3145732
  10.1 14.3 %collective-permute-start = (f32[2,2,32,256]{2,3,1,0:T(8,128)}, f32[2,2,32,256]{2,3,1,0:T(8,128)S(1)}, u32[]{:S(2)}, u32[]{:S(2)}) collective-permute-start(f32[2,2,32,256]{2,3,1,0:T(8,128)} %get-tuple-element.96), channel_id=1, source_target_pairs={{0,16},{1,17},{2,18},{3,19},{4,20},{5,21},{6,22},{7,23},{8,24},{9,... | collective-permute-start | bytes 393224 | tf_op jit(solution)/shard_map/ppermute | solution.py:24
  12.5 11.9 %collective-permute-start.1 = (f32[2,2,32,256]{2,3,1,0:T(8,128)}, f32[2,2,32,256]{2,3,1,0:T(8,128)S(1)}, u32[]{:S(2)}, u32[]{:S(2)}) collective-permute-start(f32[2,2,32,256]{2,3,1,0:T(8,128)} %get-tuple-element.97), channel_id=1, source_target_pairs={{16,0},{17,1},{18,2},{19,3},{20,4},{21,5},{22,6},{23,7},{24,8},{25... | collective-permute-start | bytes 393224 | tf_op jit(solution)/shard_map/ppermute | solution.py:26
  24.4 9.5 %copy-start.9 = (f32[2,2,32,256]{2,3,1,0:T(8,128)}, f32[2,2,32,256]{2,3,1,0:T(8,128)S(1)}, u32[]{:S(2)}) copy-start(f32[2,2,32,256]{2,3,1,0:T(8,128)S(1)} %collective-permute-done) | copy-start | bytes 393220
  24.4 9.5 %copy-start.10 = (f32[2,2,32,256]{2,3,1,0:T(8,128)}, f32[2,2,32,256]{2,3,1,0:T(8,128)S(1)}, u32[]{:S(2)}) copy-start(f32[2,2,32,256]{2,3,1,0:T(8,128)S(1)} %collective-permute-done.1) | copy-start | bytes 393220
  24.6 9.3 %collective-permute-start.2 = (f32[2,2,320,32]{2,3,1,0:T(8,128)S(1)}, f32[2,2,320,32]{2,3,1,0:T(8,128)S(1)}, u32[]{:S(2)}, u32[]{:S(2)}) collective-permute-start(f32[2,2,320,32]{2,3,1,0:T(8,128)S(1)} %get-tuple-element.84), channel_id=1, source_target_pairs={{0,1},{1,2},{2,3},{3,4},{4,5},{5,6},{6,7},{7,8},{8,9},{9,10},{10,1... | collective-permute-start | bytes 491528 | tf_op jit(solution)/shard_map/ppermute | solution.py:24
  28.8 11.2 %collective-permute-start.3 = (f32[2,2,320,32]{2,3,1,0:T(8,128)S(1)}, f32[2,2,320,32]{2,3,1,0:T(8,128)S(1)}, u32[]{:S(2)}, u32[]{:S(2)}) collective-permute-start(f32[2,2,320,32]{2,3,1,0:T(8,128)S(1)} %get-tuple-element.85), channel_id=1, source_target_pairs={{1,0},{2,1},{3,2},{4,3},{5,4},{6,5},{7,6},{8,7},{9,8},{10,9},{11,1... | collective-permute-start | bytes 491528 | tf_op jit(solution)/shard_map/ppermute | solution.py:26
  41.9 1.3 copy-start
  45.6 1.9 copy-start.1
  47.5 1.3 copy-start
  51.1 1.9 copy-start.1
  53.3 6.6 %copy-start.6 = (f32[256,256]{0,1:T(8,128)S(1)}, f32[256,256]{0,1:T(8,128)}, u32[]{:S(2)}) copy-start(f32[256,256]{0,1:T(8,128)} %copy.64) | copy-start | bytes 786436
  53.3 6.6 %copy-start.7 = (f32[256,256]{0,1:T(8,128)S(1)}, f32[256,256]{0,1:T(8,128)}, u32[]{:S(2)}) copy-start(f32[256,256]{0,1:T(8,128)} %copy.71) | copy-start | bytes 786436
  53.3 6.6 %copy-start.8 = (f32[2,2,2,256,256]{3,4,0,2,1:T(8,128)S(1)}, f32[2,2,2,256,256]{3,4,0,2,1:T(8,128)}, u32[]{:S(2)}) copy-start(f32[2,2,2,256,256]{3,4,0,2,1:T(8,128)} %get-tuple-element.57) | copy-start | bytes 6291460
  96.1 5.5 %copy-start.4 = (f32[1,1,2,256,256]{3,4,2,1,0:T(8,128)S(1)}, f32[1,1,2,256,256]{3,4,2,1,0:T(8,128)}, u32[]{:S(2)}) copy-start(f32[1,1,2,256,256]{3,4,2,1,0:T(8,128)} %copy.98) | copy-start | bytes 1572868
  148.7 1.3 copy-start.5
  182.0 9.2 %collective-permute-start.4 = (f32[2,2,32,320]{3,2,1,0:T(8,128)}, f32[2,2,32,320]{3,2,1,0:T(8,128)}, u32[]{:S(2)}, u32[]{:S(2)}) collective-permute-start(f32[2,2,32,320]{3,2,1,0:T(8,128)} %copy.124), channel_id=1, source_target_pairs={{16,0},{17,1},{18,2},{19,3},{20,4},{21,5},{22,6},{23,7},{24,8},{25... | collective-permute-start | bytes 491528 | tf_op jit(solution)/shard_map/ppermute | solution.py:13
  185.5 156.5 %all-reduce.5.cloned.1.call-start = ((), (), s32[]{:S(2)}) async-start(), calls=%async_computation.1 | async-start | bytes 1048576 | tf_op jit(solution)/shard_map/psum | solution.py:154
  186.9 12.8 %collective-permute-start.5 = (f32[2,2,32,320]{3,2,1,0:T(8,128)S(1)}, f32[2,2,32,320]{3,2,1,0:T(8,128)}, u32[]{:S(2)}, u32[]{:S(2)}) collective-permute-start(f32[2,2,32,320]{3,2,1,0:T(8,128)S(1)} %copy.126), channel_id=1, source_target_pairs={{0,16},{1,17},{2,18},{3,19},{4,20},{5,21},{6,22},{7,23},{8,24},{9,... | collective-permute-start | bytes 491528 | tf_op jit(solution)/shard_map/ppermute | solution.py:13
  204.3 6.8 %collective-permute-start.6 = (f32[2,2,32,256]{3,2,1,0:T(8,128)S(1)}, f32[2,2,32,256]{3,2,1,0:T(8,128)S(1)}, u32[]{:S(2)}, u32[]{:S(2)}) collective-permute-start(f32[2,2,32,256]{3,2,1,0:T(8,128)S(1)} %get-tuple-element.91), channel_id=1, source_target_pairs={{1,0},{2,1},{3,2},{4,3},{5,4},{6,5},{7,6},{8,7},{9,8},{10,9},{11,1... | collective-permute-start | bytes 393224 | tf_op jit(solution)/shard_map/ppermute | solution.py:13
  205.7 134.9 %copy-start.3 = (f32[2,2,256,256]{2,3,1,0:T(8,128)S(1)}, f32[2,2,256,256]{2,3,1,0:T(8,128)}, u32[]{:S(2)}) copy-start(f32[2,2,256,256]{2,3,1,0:T(8,128)} %copy-done.2) | copy-start | bytes 3145732
  205.7 91.8 %collective-permute-start.7 = (f32[2,2,32,256]{3,2,1,0:T(8,128)}, f32[2,2,32,256]{3,2,1,0:T(8,128)S(1)}, u32[]{:S(2)}, u32[]{:S(2)}) collective-permute-start(f32[2,2,32,256]{3,2,1,0:T(8,128)} %get-tuple-element.90), channel_id=1, source_target_pairs={{0,1},{1,2},{2,3},{3,4},{4,5},{5,6},{6,7},{7,8},{8,9},{9,10},{10,1... | collective-permute-start | bytes 393224 | tf_op jit(solution)/shard_map/ppermute | solution.py:13
  340.7 1.3 copy-start.11
Sparse Core Ops, SparseCore 0:
  185.7 111.8 all-reduce.2
  299.9 17.5 all-reduce.4
